TPU v7x, 32 devices: a whole 2x2x4 slice. The times are simulated.
32 devices in a mesh: group: 4 (over y, x), shard: 8 (over z, core).
Axes of the slice: x: 2, y: 2, z: 4, core: 2. Of those that a mesh axis runs over, the one named last changes fastest.
Arguments:
- grad_pooled: bfloat16 [4096, 512, 128], P(('group', 'shard')), may hold values from -6 to 6
- bag_rows: int32 [4096, 512, 8], P(('group', 'shard')), may hold values from 0 to 511
- bag_lengths: int32 [4096, 512], P(('group', 'shard')), may hold values from 1 to 8
- table_order: int32 [512], replicated, may hold values from 0 to 511, each once
- weights: bfloat16 [512, 512, 128], P('shard'), may hold values from -6 to 6
- accum: float32 [512, 512], P('shard'), may hold values from 0.1 to 10
Outputs:
- new_weights: bfloat16 [512, 512, 128], P('shard')
- new_accum: float32 [512, 512], P('shard')
All inputs are finite; a program needn't handle non-finite values.
Results may differ from a plain program's by a relative error of at most 0.001.
Values may be sent and summed in bfloat16 or wider, within the bound.
A program may use at most 128 MiB of HBM per device.

v0:
```python
import jax
import jax.numpy as jnp
from jax import lax
from jax.sharding import PartitionSpec as P

LEARN_RATE = 0.5
EPSILON = 1e-06


def expand_rows(gradient, row_ids, row_count):
    tables_first = jnp.swapaxes(gradient, 0, 1)
    picks_first = jnp.transpose(row_ids, (1, 2, 0))

    def one_table(member):
        values, chosen = member
        positions = lax.broadcasted_iota(jnp.int32, (row_count, chosen.shape[1]), 0)
        counts = jnp.zeros((row_count, chosen.shape[1]), jnp.float32)
        for column in range(chosen.shape[0]):
            counts = counts + (chosen[column][None, :] == positions).astype(jnp.float32)
        return jnp.dot(counts.astype(jnp.bfloat16), values, preferred_element_type=jnp.float32)

    return lax.map(one_table, (tables_first, picks_first))


def adagrad(weight_rows, accum_rows, row_grad):
    new_accum = accum_rows + jnp.mean(row_grad * row_grad, axis=-1)
    step_size = LEARN_RATE / (jnp.sqrt(new_accum) + EPSILON)
    new_weights = (weight_rows.astype(jnp.float32) - step_size[:, :, None] * row_grad).astype(
        jnp.bfloat16
    )
    return (new_weights, new_accum)


def body(grad_pooled, bag_rows, bag_lengths, table_order, weights, accum):
    row_count = weights.shape[1]
    bag_size = bag_rows.shape[2]
    places = lax.broadcasted_iota(jnp.int32, bag_rows.shape, 2)
    live_rows = jnp.where(places < bag_lengths[:, :, None], bag_rows, -1)
    pooled = jnp.take(grad_pooled, table_order, axis=1)
    chosen = jnp.take(live_rows, table_order, axis=1)
    groups = lax.axis_size("group")
    shards = lax.axis_size("shard")
    quarter = weights.shape[0] // groups
    samples = pooled.shape[0]
    width = pooled.shape[2]
    pooled = pooled.reshape(samples, shards, groups, quarter, width)
    pooled = jnp.transpose(pooled, (0, 2, 1, 3, 4)).reshape(
        samples, shards * groups * quarter, width
    )
    chosen = chosen.reshape(samples, shards, groups, quarter, bag_size)
    chosen = jnp.transpose(chosen, (0, 2, 1, 3, 4)).reshape(
        samples, shards * groups * quarter, bag_size
    )
    gathered = lax.all_to_all(pooled, ("group", "shard"), split_axis=1, concat_axis=0, tiled=True)
    row_ids = lax.all_to_all(chosen, ("group", "shard"), split_axis=1, concat_axis=0, tiled=True)
    row_grad = expand_rows(gathered, row_ids, row_count)
    start = lax.axis_index("group") * quarter
    weight_part = lax.dynamic_slice_in_dim(weights, start, quarter, 0)
    accum_part = lax.dynamic_slice_in_dim(accum, start, quarter, 0)
    part_weights, part_accum = adagrad(weight_part, accum_part, row_grad)
    full_weights, full_accum = (
        lax.all_gather(part_weights.astype(jnp.float32), "group", axis=0, tiled=True),
        lax.all_gather(part_accum, "group", axis=0, tiled=True),
    )
    return (full_weights.astype(jnp.bfloat16), full_accum)


def solution(mesh):
    in_specs = (
        P(("group", "shard"), None, None),
        P(("group", "shard"), None, None),
        P(("group", "shard"), None),
        P(),
        P("shard", None, None),
        P("shard", None),
    )
    out_specs = (P("shard", None, None), P("shard", None))
    return jax.shard_map(body, mesh=mesh, in_specs=in_specs, out_specs=out_specs, check_vma=False)
```

profile of v0, /device:TPU:0, one launch (start us, length us, event | category | flops | bytes accessed | tf_op | source)
XLA Modules:
  0.0 827.4 jit_solution(13259575028350120470)
XLA Ops:
  8.6 3.1 copy.22
  12.8 1.8 fusion.7
  14.6 2.7 gather_fusion
  17.3 1.9 select_bitcast_fusion
  20.7 7.3 all-to-all-start
  28.1 55.3 %gather_fusion.1 = bf16[512,128,128]{2,0,1:T(8,128)(2,1)} fusion(bf16[128,512,128]{2,1,0:T(8,128)(2,1)} %param.8, s32[1024]{0:T(1024)S(1)} %pad_clamp_fusion), kind=kCustom, calls=%fused_computation.1 | custom fusion | bytes 33556480 | tf_op jit(solution)/shard_map/jit(_take)/gather | solution.py:39
  83.4 9.1 %copy_select_fusion = bf16[128,8,4,16,128]{4,3,1,2,0:T(8,128)(2,1)S(1)} fusion(bf16[128,8,4,16,128]{4,3,2,1,0:T(8,128)(2,1)} %bitcast.64, pred[8,4,16]{2,0,1:T(8,128)(4,1)S(1)} %copy.25), kind=kLoop, calls=%fused_computation.25 | loop fusion | flops 8388608 | bytes 33554944 | tf_op jit(solution)/shard_map/jit(_take)/select_n | solution.py:39
  92.5 38.2 %copy.27 = bf16[128,512,128]{2,0,1:T(8,128)(2,1)} copy(bf16[128,512,128]{2,1,0:T(8,128)(2,1)S(1)} %bitcast.65) | data formatting | bytes 33554432 | tf_op jit(solution)/shard_map/reshape | solution.py:47
  130.6 6.0 all-to-all-start.1
  138.2 362.9 %all-to-all-done.1 = bf16[128,512,128]{2,0,1:T(8,128)(2,1)} async-done(((bf16[128,512,128]{2,0,1:T(8,128)(2,1)}), bf16[128,512,128]{2,0,1:T(8,128)(2,1)}, u32[]{:S(2)}, u32[]{:S(2)}) %all-to-all-start.1) | async-done | bytes 16777248 | tf_op jit(solution)/shard_map/all_to_all | solution.py:54
  501.1 15.2 %copy.29 = bf16[32,128,16,128]{3,2,1,0:T(8,128)(2,1)S(1)} copy(bf16[32,128,16,128]{3,1,2,0:T(8,128)(2,1)} %bitcast.23) | data formatting | bytes 33554432 | tf_op jit(solution)/shard_map/all_to_all | solution.py:54
  516.4 11.9 %copy.30 = bf16[16,4096,128]{2,1,0:T(8,128)(2,1)} copy(bf16[16,4096,128]{2,0,1:T(8,128)(2,1)S(1)} %bitcast.66) | data formatting | bytes 33554432 | tf_op jit(solution)/shard_map/while | solution.py:22
  528.3 190.0 %while.10 = (s32[]{:T(128)}, f32[16,512,128]{2,1,0:T(8,128)}, s32[16,8,4096]{2,1,0:T(8,128)}, bf16[16,4096,128]{2,1,0:T(8,128)(2,1)}, s32[]{:T(128)}, /*index=5*...) while((s32[]{:T(128)}, f32[16,512,128]{2,1,0:T(8,128)}, s32[16,8,4096]{2,1,0:T(8,128)}, ...), condition=%wide.region_1.2_spmd, body=%wide.region_0.1_spmd.sunk | while | flops 587202560 | bytes 1705201 | solution.py:22
  529.9 10.2 %fusion.11 = f32[16,512,128]{2,1,0:T(8,128)} fusion(f32[16,512,128]{2,1,0:T(8,128)} %get-tuple-element.106, s32[]{:T(128)} %get-tuple-element.105, s32[4096]{0:T(1024)S(1)} %bitcast.77, s32[4096]{0:T(1024)S(1)} %bitcast.71, s32[4096]{0:T(1024)S(1)} %bitcast.72, s32[4096]{0:T(1024)S(1)} %bitcast.73, s32[4096]{0:T(1024)S(1)} %bitcast.74, ...), kind=kOutput, calls=%fused_computation.13.clone.1 | convolution fusion | flops 587202560 | bytes 1442816 | tf_op jit(solution)/shard_map/while/body/eval_jaxpr/dot_general | solution.py:20
  540.1 1.6 constant_dynamic-slice_fusion.9
  541.7 10.2 %fusion.11 = f32[16,512,128]{2,1,0:T(8,128)} fusion(f32[16,512,128]{2,1,0:T(8,128)} %get-tuple-element.106, s32[]{:T(128)} %get-tuple-element.105, s32[4096]{0:T(1024)S(1)} %bitcast.77, s32[4096]{0:T(1024)S(1)} %bitcast.71, s32[4096]{0:T(1024)S(1)} %bitcast.72, s32[4096]{0:T(1024)S(1)} %bitcast.73, s32[4096]{0:T(1024)S(1)} %bitcast.74, ...), kind=kOutput, calls=%fused_computation.13.clone.1 | convolution fusion | flops 587202560 | bytes 1442816 | tf_op jit(solution)/shard_map/while/body/eval_jaxpr/dot_general | solution.py:20
  551.9 1.9 constant_dynamic-slice_fusion.9
  553.8 10.2 %fusion.11 = f32[16,512,128]{2,1,0:T(8,128)} fusion(f32[16,512,128]{2,1,0:T(8,128)} %get-tuple-element.106, s32[]{:T(128)} %get-tuple-element.105, s32[4096]{0:T(1024)S(1)} %bitcast.77, s32[4096]{0:T(1024)S(1)} %bitcast.71, s32[4096]{0:T(1024)S(1)} %bitcast.72, s32[4096]{0:T(1024)S(1)} %bitcast.73, s32[4096]{0:T(1024)S(1)} %bitcast.74, ...), kind=kOutput, calls=%fused_computation.13.clone.1 | convolution fusion | flops 587202560 | bytes 1442816 | tf_op jit(solution)/shard_map/while/body/eval_jaxpr/dot_general | solution.py:20
  564.0 1.6 constant_dynamic-slice_fusion.9
  565.6 10.2 %fusion.11 = f32[16,512,128]{2,1,0:T(8,128)} fusion(f32[16,512,128]{2,1,0:T(8,128)} %get-tuple-element.106, s32[]{:T(128)} %get-tuple-element.105, s32[4096]{0:T(1024)S(1)} %bitcast.77, s32[4096]{0:T(1024)S(1)} %bitcast.71, s32[4096]{0:T(1024)S(1)} %bitcast.72, s32[4096]{0:T(1024)S(1)} %bitcast.73, s32[4096]{0:T(1024)S(1)} %bitcast.74, ...), kind=kOutput, calls=%fused_computation.13.clone.1 | convolution fusion | flops 587202560 | bytes 1442816 | tf_op jit(solution)/shard_map/while/body/eval_jaxpr/dot_general | solution.py:20
  575.8 1.6 constant_dynamic-slice_fusion.9
  577.4 10.2 %fusion.11 = f32[16,512,128]{2,1,0:T(8,128)} fusion(f32[16,512,128]{2,1,0:T(8,128)} %get-tuple-element.106, s32[]{:T(128)} %get-tuple-element.105, s32[4096]{0:T(1024)S(1)} %bitcast.77, s32[4096]{0:T(1024)S(1)} %bitcast.71, s32[4096]{0:T(1024)S(1)} %bitcast.72, s32[4096]{0:T(1024)S(1)} %bitcast.73, s32[4096]{0:T(1024)S(1)} %bitcast.74, ...), kind=kOutput, calls=%fused_computation.13.clone.1 | convolution fusion | flops 587202560 | bytes 1442816 | tf_op jit(solution)/shard_map/while/body/eval_jaxpr/dot_general | solution.py:20
  587.6 1.9 constant_dynamic-slice_fusion.9
  589.5 10.2 %fusion.11 = f32[16,512,128]{2,1,0:T(8,128)} fusion(f32[16,512,128]{2,1,0:T(8,128)} %get-tuple-element.106, s32[]{:T(128)} %get-tuple-element.105, s32[4096]{0:T(1024)S(1)} %bitcast.77, s32[4096]{0:T(1024)S(1)} %bitcast.71, s32[4096]{0:T(1024)S(1)} %bitcast.72, s32[4096]{0:T(1024)S(1)} %bitcast.73, s32[4096]{0:T(1024)S(1)} %bitcast.74, ...), kind=kOutput, calls=%fused_computation.13.clone.1 | convolution fusion | flops 587202560 | bytes 1442816 | tf_op jit(solution)/shard_map/while/body/eval_jaxpr/dot_general | solution.py:20
  599.7 1.6 constant_dynamic-slice_fusion.9
  601.3 10.2 %fusion.11 = f32[16,512,128]{2,1,0:T(8,128)} fusion(f32[16,512,128]{2,1,0:T(8,128)} %get-tuple-element.106, s32[]{:T(128)} %get-tuple-element.105, s32[4096]{0:T(1024)S(1)} %bitcast.77, s32[4096]{0:T(1024)S(1)} %bitcast.71, s32[4096]{0:T(1024)S(1)} %bitcast.72, s32[4096]{0:T(1024)S(1)} %bitcast.73, s32[4096]{0:T(1024)S(1)} %bitcast.74, ...), kind=kOutput, calls=%fused_computation.13.clone.1 | convolution fusion | flops 587202560 | bytes 1442816 | tf_op jit(solution)/shard_map/while/body/eval_jaxpr/dot_general | solution.py:20
  611.5 1.6 constant_dynamic-slice_fusion.9
  613.1 10.2 %fusion.11 = f32[16,512,128]{2,1,0:T(8,128)} fusion(f32[16,512,128]{2,1,0:T(8,128)} %get-tuple-element.106, s32[]{:T(128)} %get-tuple-element.105, s32[4096]{0:T(1024)S(1)} %bitcast.77, s32[4096]{0:T(1024)S(1)} %bitcast.71, s32[4096]{0:T(1024)S(1)} %bitcast.72, s32[4096]{0:T(1024)S(1)} %bitcast.73, s32[4096]{0:T(1024)S(1)} %bitcast.74, ...), kind=kOutput, calls=%fused_computation.13.clone.1 | convolution fusion | flops 587202560 | bytes 1442816 | tf_op jit(solution)/shard_map/while/body/eval_jaxpr/dot_general | solution.py:20
  623.3 1.9 constant_dynamic-slice_fusion.9
  625.1 10.2 %fusion.11 = f32[16,512,128]{2,1,0:T(8,128)} fusion(f32[16,512,128]{2,1,0:T(8,128)} %get-tuple-element.106, s32[]{:T(128)} %get-tuple-element.105, s32[4096]{0:T(1024)S(1)} %bitcast.77, s32[4096]{0:T(1024)S(1)} %bitcast.71, s32[4096]{0:T(1024)S(1)} %bitcast.72, s32[4096]{0:T(1024)S(1)} %bitcast.73, s32[4096]{0:T(1024)S(1)} %bitcast.74, ...), kind=kOutput, calls=%fused_computation.13.clone.1 | convolution fusion | flops 587202560 | bytes 1442816 | tf_op jit(solution)/shard_map/while/body/eval_jaxpr/dot_general | solution.py:20
  636.9 10.2 %fusion.11 = f32[16,512,128]{2,1,0:T(8,128)} fusion(f32[16,512,128]{2,1,0:T(8,128)} %get-tuple-element.106, s32[]{:T(128)} %get-tuple-element.105, s32[4096]{0:T(1024)S(1)} %bitcast.77, s32[4096]{0:T(1024)S(1)} %bitcast.71, s32[4096]{0:T(1024)S(1)} %bitcast.72, s32[4096]{0:T(1024)S(1)} %bitcast.73, s32[4096]{0:T(1024)S(1)} %bitcast.74, ...), kind=kOutput, calls=%fused_computation.13.clone.1 | convolution fusion | flops 587202560 | bytes 1442816 | tf_op jit(solution)/shard_map/while/body/eval_jaxpr/dot_general | solution.py:20
  647.1 1.6 constant_dynamic-slice_fusion.9
  648.7 10.2 %fusion.11 = f32[16,512,128]{2,1,0:T(8,128)} fusion(f32[16,512,128]{2,1,0:T(8,128)} %get-tuple-element.106, s32[]{:T(128)} %get-tuple-element.105, s32[4096]{0:T(1024)S(1)} %bitcast.77, s32[4096]{0:T(1024)S(1)} %bitcast.71, s32[4096]{0:T(1024)S(1)} %bitcast.72, s32[4096]{0:T(1024)S(1)} %bitcast.73, s32[4096]{0:T(1024)S(1)} %bitcast.74, ...), kind=kOutput, calls=%fused_computation.13.clone.1 | convolution fusion | flops 587202560 | bytes 1442816 | tf_op jit(solution)/shard_map/while/body/eval_jaxpr/dot_general | solution.py:20
  658.9 1.6 constant_dynamic-slice_fusion.9
  660.6 10.2 %fusion.11 = f32[16,512,128]{2,1,0:T(8,128)} fusion(f32[16,512,128]{2,1,0:T(8,128)} %get-tuple-element.106, s32[]{:T(128)} %get-tuple-element.105, s32[4096]{0:T(1024)S(1)} %bitcast.77, s32[4096]{0:T(1024)S(1)} %bitcast.71, s32[4096]{0:T(1024)S(1)} %bitcast.72, s32[4096]{0:T(1024)S(1)} %bitcast.73, s32[4096]{0:T(1024)S(1)} %bitcast.74, ...), kind=kOutput, calls=%fused_computation.13.clone.1 | convolution fusion | flops 587202560 | bytes 1442816 | tf_op jit(solution)/shard_map/while/body/eval_jaxpr/dot_general | solution.py:20
  670.7 1.6 constant_dynamic-slice_fusion.9
  672.4 10.2 %fusion.11 = f32[16,512,128]{2,1,0:T(8,128)} fusion(f32[16,512,128]{2,1,0:T(8,128)} %get-tuple-element.106, s32[]{:T(128)} %get-tuple-element.105, s32[4096]{0:T(1024)S(1)} %bitcast.77, s32[4096]{0:T(1024)S(1)} %bitcast.71, s32[4096]{0:T(1024)S(1)} %bitcast.72, s32[4096]{0:T(1024)S(1)} %bitcast.73, s32[4096]{0:T(1024)S(1)} %bitcast.74, ...), kind=kOutput, calls=%fused_computation.13.clone.1 | convolution fusion | flops 587202560 | bytes 1442816 | tf_op jit(solution)/shard_map/while/body/eval_jaxpr/dot_general | solution.py:20
  682.6 1.6 constant_dynamic-slice_fusion.9
  684.2 10.2 %fusion.11 = f32[16,512,128]{2,1,0:T(8,128)} fusion(f32[16,512,128]{2,1,0:T(8,128)} %get-tuple-element.106, s32[]{:T(128)} %get-tuple-element.105, s32[4096]{0:T(1024)S(1)} %bitcast.77, s32[4096]{0:T(1024)S(1)} %bitcast.71, s32[4096]{0:T(1024)S(1)} %bitcast.72, s32[4096]{0:T(1024)S(1)} %bitcast.73, s32[4096]{0:T(1024)S(1)} %bitcast.74, ...), kind=kOutput, calls=%fused_computation.13.clone.1 | convolution fusion | flops 587202560 | bytes 1442816 | tf_op jit(solution)/shard_map/while/body/eval_jaxpr/dot_general | solution.py:20
  694.4 1.9 constant_dynamic-slice_fusion.9
  696.3 10.2 %fusion.11 = f32[16,512,128]{2,1,0:T(8,128)} fusion(f32[16,512,128]{2,1,0:T(8,128)} %get-tuple-element.106, s32[]{:T(128)} %get-tuple-element.105, s32[4096]{0:T(1024)S(1)} %bitcast.77, s32[4096]{0:T(1024)S(1)} %bitcast.71, s32[4096]{0:T(1024)S(1)} %bitcast.72, s32[4096]{0:T(1024)S(1)} %bitcast.73, s32[4096]{0:T(1024)S(1)} %bitcast.74, ...), kind=kOutput, calls=%fused_computation.13.clone.1 | convolution fusion | flops 587202560 | bytes 1442816 | tf_op jit(solution)/shard_map/while/body/eval_jaxpr/dot_general | solution.py:20
  706.5 1.6 constant_dynamic-slice_fusion.9
  708.1 10.2 %fusion.11 = f32[16,512,128]{2,1,0:T(8,128)} fusion(f32[16,512,128]{2,1,0:T(8,128)} %get-tuple-element.106, s32[]{:T(128)} %get-tuple-element.105, s32[4096]{0:T(1024)S(1)} %bitcast.77, s32[4096]{0:T(1024)S(1)} %bitcast.71, s32[4096]{0:T(1024)S(1)} %bitcast.72, s32[4096]{0:T(1024)S(1)} %bitcast.73, s32[4096]{0:T(1024)S(1)} %bitcast.74, ...), kind=kOutput, calls=%fused_computation.13.clone.1 | convolution fusion | flops 587202560 | bytes 1442816 | tf_op jit(solution)/shard_map/while/body/eval_jaxpr/dot_general | solution.py:20
  718.3 3.3 multiply_reduce_fusion
  722.4 4.4 fusion.6
  726.8 7.5 all_gather.7
  734.3 77.8 %all-gather.2.cloned.1.call-done = bf16[64,512,128]{2,1,0:T(8,128)(2,1)} async-done(((bf16[16,512,128]{2,1,0:T(8,128)(2,1)}), bf16[64,512,128]{2,1,0:T(8,128)(2,1)}) %all-gather.2.cloned.1.call-update) | async-done | bytes 8388624 | tf_op jit(solution)/shard_map/all_gather | solution.py:62
  812.1 7.8 copy.45
  (16 shorter events, 10.3 us)
Async XLA Ops:
  20.7 109.9 %all-to-all-start = ((s32[128,512,8]{0,2,1:T(8,128)}), s32[128,512,8]{0,2,1:T(8,128)S(1)}, u32[]{:S(2)}, u32[]{:S(2)}) async-start(s32[128,512,8]{0,2,1:T(8,128)} %bitcast.68), calls=%async_computation | async-start | bytes 4194304 | tf_op jit(solution)/shard_map/all_to_all | solution.py:55
  130.6 370.5 %all-to-all-start.1 = ((bf16[128,512,128]{2,0,1:T(8,128)(2,1)}), bf16[128,512,128]{2,0,1:T(8,128)(2,1)}, u32[]{:S(2)}, u32[]{:S(2)}) async-start(bf16[128,512,128]{2,0,1:T(8,128)(2,1)} %copy.27), calls=%async_computation.1 | async-start | bytes 33554432 | tf_op jit(solution)/shard_map/all_to_all | solution.py:54
  136.6 675.5 %all-gather.2.cloned.1.call-start = ((), (), s32[]{:S(2)}) async-start(), calls=%async_computation.2 | async-start | bytes 10485760 | tf_op jit(solution)/shard_map/all_gather | solution.py:62
Sparse Core Ops, SparseCore 0:
  727.0 85.1 all-gather.1
where the time goes:
time: 829 us; the launch traced here: 827 us
  waiting for transfers between devices  441 us (53%)
  local copies, waits for them, and re-layouts  166 us (20%)
  matrix products  163 us (20%)
  other arithmetic  22.7 us (3%)
  between operations  14.1 us (2%)
  starting transfers between devices  13.3 us (2%)
    all_to_all x1, waiting for transfers between devices, body(): lax.all_to_all(pooled, ('group', 'shard'), split_axis=1, concat_axis=0, t...  363 us
    dot_general x16, matrix products, one_table(): jnp.dot(counts.astype(jnp.bfloat16), values, preferred_element_type=jnp.f...  163 us
    all_gather x1, waiting for transfers between devices, body(): lax.all_gather(part_weights.astype(jnp.float32), 'group', axis=0, tiled=T...  77.8 us
    gather x1, local copies, waits for them, and re-layouts, body(): pooled = jnp.take(grad_pooled, table_order, axis=1)  55.3 us
    reshape x1, local copies, waits for them, and re-layouts, body(): jnp.transpose(pooled, (0, 2, 1, 3, 4))  38.2 us
    slice x16, local copies, waits for them, and re-layouts, one_table(): counts = counts + (chosen[column][None, :] == positions).astype(jnp.float32)  26.8 us
  transfers between devices with their start and end apart: 3, of which 2 were waited for; matrix products, arithmetic and copies ran while one was open for 13% of the time, Pallas kernels for 0%

commit v1 on v0

--- a/solution.py
+++ b/solution.py
@@ -51,7 +51,15 @@
     chosen = jnp.transpose(chosen, (0, 2, 1, 3, 4)).reshape(
         samples, shards * groups * quarter, bag_size
     )
-    gathered = lax.all_to_all(pooled, ("group", "shard"), split_axis=1, concat_axis=0, tiled=True)
+    gathered = jnp.concatenate(
+        lax.all_to_all(
+            jnp.stack(jnp.split(pooled, lax.axis_size(("group", "shard")), axis=1)),
+            ("group", "shard"),
+            0,
+            0,
+        ),
+        axis=0,
+    )
     row_ids = lax.all_to_all(chosen, ("group", "shard"), split_axis=1, concat_axis=0, tiled=True)
     row_grad = expand_rows(gathered, row_ids, row_count)
     start = lax.axis_index("group") * quarter

time: 829 us -> 807 us (0.973)
  local copies, waits for them, and re-layouts: 166 us -> 144 us
    unnamed x4 -> x35, local copies, waits for them, and re-layouts: 12.6 us -> 39.7 us
    reshape x1, local copies, waits for them, and re-layouts: 38.2 us -> 15.1 us  [body(): jnp.concatenate(lax.all_to_all(jnp.stack(jnp.split(pooled, lax.axis_size(...]
    all_to_all x1 -> x0, local copies, waits for them, and re-layouts: 15.2 us -> none  [body(): lax.all_to_all(pooled, ('group', 'shard'), split_axis=1, concat_axis=0, t...]
    while x1 -> x0, local copies, waits for them, and re-layouts: 11.9 us -> none  [expand_rows(): return lax.map(one_table, (tables_first, picks_first))]
  transfers between devices with their start and end apart: 3 -> 3, of which waited for: 2 -> 2; matrix products, arithmetic and copies ran while one was open for 13% -> 12% of each run, Pallas kernels for 0% -> 0%
where the time goes in v1:
time: 807 us; the launch traced here: 805 us
  waiting for transfers between devices  441 us (55%)
  matrix products  163 us (20%)
  local copies, waits for them, and re-layouts  144 us (18%)
  other arithmetic  22.9 us (3%)
  between operations  14.1 us (2%)
  starting transfers between devices  13.3 us (2%)
    all_to_all x1, waiting for transfers between devices, body(): lax.all_to_all(jnp.stack(jnp.split(pooled, lax.axis_size(('group', 'shard...  363 us
    dot_general x16, matrix products, one_table(): jnp.dot(counts.astype(jnp.bfloat16), values, preferred_element_type=jnp.f...  163 us
    all_gather x1, waiting for transfers between devices, body(): lax.all_gather(part_weights.astype(jnp.float32), 'group', axis=0, tiled=T...  77.8 us
    gather x1, local copies, waits for them, and re-layouts, body(): pooled = jnp.take(grad_pooled, table_order, axis=1)  55.3 us
    unnamed x35, local copies, waits for them, and re-layouts  39.7 us
    slice x16, local copies, waits for them, and re-layouts, one_table(): counts = counts + (chosen[column][None, :] == positions).astype(jnp.float32)  26.8 us
  transfers between devices with their start and end apart: 3, of which 2 were waited for; matrix products, arithmetic and copies ran while one was open for 12% of the time, Pallas kernels for 0%

profile of v1, /device:TPU:0, one launch (start us, length us, event | category | flops | bytes accessed | tf_op | source)
XLA Modules:
  0.0 805.4 jit_solution(18384485396412939239)
XLA Ops:
  8.6 3.1 copy.82
  12.8 1.8 fusion.7
  14.6 2.7 gather_fusion
  17.3 1.9 select_bitcast_fusion
  20.7 7.3 all-to-all-start
  28.1 55.3 %gather_fusion.1 = bf16[512,128,128]{2,0,1:T(8,128)(2,1)} fusion(bf16[128,512,128]{2,1,0:T(8,128)(2,1)} %param.8, s32[1024]{0:T(1024)S(1)} %pad_clamp_fusion), kind=kCustom, calls=%fused_computation.1 | custom fusion | bytes 33556480 | tf_op jit(solution)/shard_map/jit(_take)/gather | solution.py:39
  83.4 9.3 %copy_select_fusion = bf16[128,8,4,16,128]{4,3,1,2,0:T(8,128)(2,1)S(1)} fusion(bf16[128,8,4,16,128]{4,3,2,1,0:T(8,128)(2,1)} %bitcast.222, pred[8,4,16]{2,0,1:T(8,128)(4,1)S(1)} %copy.85), kind=kLoop, calls=%fused_computation.26 | loop fusion | flops 8388608 | bytes 33554944 | tf_op jit(solution)/shard_map/jit(_take)/select_n | solution.py:39
  120.7 6.0 all-to-all-start.1
  128.2 362.9 %all-to-all-done.1 = bf16[32,128,16,128]{3,2,1,0:T(8,128)(2,1)} async-done(((bf16[32,128,16,128]{3,2,1,0:T(8,128)(2,1)}), bf16[32,128,16,128]{3,2,1,0:T(8,128)(2,1)}, u32[]{:S(2)}, u32[]{:S(2)}) %all-to-all-start.1) | async-done | bytes 16777248 | tf_op jit(solution)/shard_map/all_to_all | solution.py:55
  491.2 15.1 %copy.92 = bf16[4096,16,128]{2,0,1:T(8,128)(2,1)} copy(bf16[4096,16,128]{2,1,0:T(8,128)(2,1)} %bitcast.54) | data formatting | bytes 33554432 | tf_op jit(solution)/shard_map/reshape | solution.py:54
  506.3 190.0 %while.10 = (s32[]{:T(128)}, f32[16,512,128]{2,1,0:T(8,128)}, s32[16,8,4096]{2,1,0:T(8,128)}, bf16[16,4096,128]{2,1,0:T(8,128)(2,1)}, s32[]{:T(128)}, /*index=5*...) while((s32[]{:T(128)}, f32[16,512,128]{2,1,0:T(8,128)}, s32[16,8,4096]{2,1,0:T(8,128)}, ...), condition=%wide.region_1.2_spmd, body=%wide.region_0.1_spmd.sunk | while | flops 587202560 | bytes 1705201 | solution.py:22
  506.3 1.6 constant_dynamic-slice_fusion.9
  507.9 10.2 %fusion.43 = f32[16,512,128]{2,1,0:T(8,128)} fusion(f32[16,512,128]{2,1,0:T(8,128)} %get-tuple-element.98, s32[]{:T(128)} %get-tuple-element.97, s32[4096]{0:T(1024)S(1)} %bitcast.234, s32[4096]{0:T(1024)S(1)} %bitcast.228, s32[4096]{0:T(1024)S(1)} %bitcast.229, s32[4096]{0:T(1024)S(1)} %bitcast.230, s32[4096]{0:T(1024)S(1)} %bitcast.231, ...), kind=kOutput, calls=%fused_computation.13.clone.1 | convolution fusion | flops 587202560 | bytes 1442816 | tf_op jit(solution)/shard_map/while/body/eval_jaxpr/dot_general | solution.py:20
  518.1 1.6 constant_dynamic-slice_fusion.9
  519.7 10.2 %fusion.43 = f32[16,512,128]{2,1,0:T(8,128)} fusion(f32[16,512,128]{2,1,0:T(8,128)} %get-tuple-element.98, s32[]{:T(128)} %get-tuple-element.97, s32[4096]{0:T(1024)S(1)} %bitcast.234, s32[4096]{0:T(1024)S(1)} %bitcast.228, s32[4096]{0:T(1024)S(1)} %bitcast.229, s32[4096]{0:T(1024)S(1)} %bitcast.230, s32[4096]{0:T(1024)S(1)} %bitcast.231, ...), kind=kOutput, calls=%fused_computation.13.clone.1 | convolution fusion | flops 587202560 | bytes 1442816 | tf_op jit(solution)/shard_map/while/body/eval_jaxpr/dot_general | solution.py:20
  529.9 1.9 constant_dynamic-slice_fusion.9
  531.8 10.2 %fusion.43 = f32[16,512,128]{2,1,0:T(8,128)} fusion(f32[16,512,128]{2,1,0:T(8,128)} %get-tuple-element.98, s32[]{:T(128)} %get-tuple-element.97, s32[4096]{0:T(1024)S(1)} %bitcast.234, s32[4096]{0:T(1024)S(1)} %bitcast.228, s32[4096]{0:T(1024)S(1)} %bitcast.229, s32[4096]{0:T(1024)S(1)} %bitcast.230, s32[4096]{0:T(1024)S(1)} %bitcast.231, ...), kind=kOutput, calls=%fused_computation.13.clone.1 | convolution fusion | flops 587202560 | bytes 1442816 | tf_op jit(solution)/shard_map/while/body/eval_jaxpr/dot_general | solution.py:20
  542.0 1.6 constant_dynamic-slice_fusion.9
  543.6 10.2 %fusion.43 = f32[16,512,128]{2,1,0:T(8,128)} fusion(f32[16,512,128]{2,1,0:T(8,128)} %get-tuple-element.98, s32[]{:T(128)} %get-tuple-element.97, s32[4096]{0:T(1024)S(1)} %bitcast.234, s32[4096]{0:T(1024)S(1)} %bitcast.228, s32[4096]{0:T(1024)S(1)} %bitcast.229, s32[4096]{0:T(1024)S(1)} %bitcast.230, s32[4096]{0:T(1024)S(1)} %bitcast.231, ...), kind=kOutput, calls=%fused_computation.13.clone.1 | convolution fusion | flops 587202560 | bytes 1442816 | tf_op jit(solution)/shard_map/while/body/eval_jaxpr/dot_general | solution.py:20
  553.8 1.6 constant_dynamic-slice_fusion.9
  555.4 10.2 %fusion.43 = f32[16,512,128]{2,1,0:T(8,128)} fusion(f32[16,512,128]{2,1,0:T(8,128)} %get-tuple-element.98, s32[]{:T(128)} %get-tuple-element.97, s32[4096]{0:T(1024)S(1)} %bitcast.234, s32[4096]{0:T(1024)S(1)} %bitcast.228, s32[4096]{0:T(1024)S(1)} %bitcast.229, s32[4096]{0:T(1024)S(1)} %bitcast.230, s32[4096]{0:T(1024)S(1)} %bitcast.231, ...), kind=kOutput, calls=%fused_computation.13.clone.1 | convolution fusion | flops 587202560 | bytes 1442816 | tf_op jit(solution)/shard_map/while/body/eval_jaxpr/dot_general | solution.py:20
  565.6 1.9 constant_dynamic-slice_fusion.9
  567.4 10.2 %fusion.43 = f32[16,512,128]{2,1,0:T(8,128)} fusion(f32[16,512,128]{2,1,0:T(8,128)} %get-tuple-element.98, s32[]{:T(128)} %get-tuple-element.97, s32[4096]{0:T(1024)S(1)} %bitcast.234, s32[4096]{0:T(1024)S(1)} %bitcast.228, s32[4096]{0:T(1024)S(1)} %bitcast.229, s32[4096]{0:T(1024)S(1)} %bitcast.230, s32[4096]{0:T(1024)S(1)} %bitcast.231, ...), kind=kOutput, calls=%fused_computation.13.clone.1 | convolution fusion | flops 587202560 | bytes 1442816 | tf_op jit(solution)/shard_map/while/body/eval_jaxpr/dot_general | solution.py:20
  577.6 1.6 constant_dynamic-slice_fusion.9
  579.2 10.2 %fusion.43 = f32[16,512,128]{2,1,0:T(8,128)} fusion(f32[16,512,128]{2,1,0:T(8,128)} %get-tuple-element.98, s32[]{:T(128)} %get-tuple-element.97, s32[4096]{0:T(1024)S(1)} %bitcast.234, s32[4096]{0:T(1024)S(1)} %bitcast.228, s32[4096]{0:T(1024)S(1)} %bitcast.229, s32[4096]{0:T(1024)S(1)} %bitcast.230, s32[4096]{0:T(1024)S(1)} %bitcast.231, ...), kind=kOutput, calls=%fused_computation.13.clone.1 | convolution fusion | flops 587202560 | bytes 1442816 | tf_op jit(solution)/shard_map/while/body/eval_jaxpr/dot_general | solution.py:20
  589.4 1.6 constant_dynamic-slice_fusion.9
  591.1 10.2 %fusion.43 = f32[16,512,128]{2,1,0:T(8,128)} fusion(f32[16,512,128]{2,1,0:T(8,128)} %get-tuple-element.98, s32[]{:T(128)} %get-tuple-element.97, s32[4096]{0:T(1024)S(1)} %bitcast.234, s32[4096]{0:T(1024)S(1)} %bitcast.228, s32[4096]{0:T(1024)S(1)} %bitcast.229, s32[4096]{0:T(1024)S(1)} %bitcast.230, s32[4096]{0:T(1024)S(1)} %bitcast.231, ...), kind=kOutput, calls=%fused_computation.13.clone.1 | convolution fusion | flops 587202560 | bytes 1442816 | tf_op jit(solution)/shard_map/while/body/eval_jaxpr/dot_general | solution.py:20
  601.2 1.9 constant_dynamic-slice_fusion.9
  603.1 10.2 %fusion.43 = f32[16,512,128]{2,1,0:T(8,128)} fusion(f32[16,512,128]{2,1,0:T(8,128)} %get-tuple-element.98, s32[]{:T(128)} %get-tuple-element.97, s32[4096]{0:T(1024)S(1)} %bitcast.234, s32[4096]{0:T(1024)S(1)} %bitcast.228, s32[4096]{0:T(1024)S(1)} %bitcast.229, s32[4096]{0:T(1024)S(1)} %bitcast.230, s32[4096]{0:T(1024)S(1)} %bitcast.231, ...), kind=kOutput, calls=%fused_computation.13.clone.1 | convolution fusion | flops 587202560 | bytes 1442816 | tf_op jit(solution)/shard_map/while/body/eval_jaxpr/dot_general | solution.py:20
  613.3 1.6 constant_dynamic-slice_fusion.9
  614.9 10.2 %fusion.43 = f32[16,512,128]{2,1,0:T(8,128)} fusion(f32[16,512,128]{2,1,0:T(8,128)} %get-tuple-element.98, s32[]{:T(128)} %get-tuple-element.97, s32[4096]{0:T(1024)S(1)} %bitcast.234, s32[4096]{0:T(1024)S(1)} %bitcast.228, s32[4096]{0:T(1024)S(1)} %bitcast.229, s32[4096]{0:T(1024)S(1)} %bitcast.230, s32[4096]{0:T(1024)S(1)} %bitcast.231, ...), kind=kOutput, calls=%fused_computation.13.clone.1 | convolution fusion | flops 587202560 | bytes 1442816 | tf_op jit(solution)/shard_map/while/body/eval_jaxpr/dot_general | solution.py:20
  625.1 1.6 constant_dynamic-slice_fusion.9
  626.7 10.2 %fusion.43 = f32[16,512,128]{2,1,0:T(8,128)} fusion(f32[16,512,128]{2,1,0:T(8,128)} %get-tuple-element.98, s32[]{:T(128)} %get-tuple-element.97, s32[4096]{0:T(1024)S(1)} %bitcast.234, s32[4096]{0:T(1024)S(1)} %bitcast.228, s32[4096]{0:T(1024)S(1)} %bitcast.229, s32[4096]{0:T(1024)S(1)} %bitcast.230, s32[4096]{0:T(1024)S(1)} %bitcast.231, ...), kind=kOutput, calls=%fused_computation.13.clone.1 | convolution fusion | flops 587202560 | bytes 1442816 | tf_op jit(solution)/shard_map/while/body/eval_jaxpr/dot_general | solution.py:20
  636.9 1.6 constant_dynamic-slice_fusion.9
  638.5 10.2 %fusion.43 = f32[16,512,128]{2,1,0:T(8,128)} fusion(f32[16,512,128]{2,1,0:T(8,128)} %get-tuple-element.98, s32[]{:T(128)} %get-tuple-element.97, s32[4096]{0:T(1024)S(1)} %bitcast.234, s32[4096]{0:T(1024)S(1)} %bitcast.228, s32[4096]{0:T(1024)S(1)} %bitcast.229, s32[4096]{0:T(1024)S(1)} %bitcast.230, s32[4096]{0:T(1024)S(1)} %bitcast.231, ...), kind=kOutput, calls=%fused_computation.13.clone.1 | convolution fusion | flops 587202560 | bytes 1442816 | tf_op jit(solution)/shard_map/while/body/eval_jaxpr/dot_general | solution.py:20
  648.7 1.6 constant_dynamic-slice_fusion.9
  650.3 10.2 %fusion.43 = f32[16,512,128]{2,1,0:T(8,128)} fusion(f32[16,512,128]{2,1,0:T(8,128)} %get-tuple-element.98, s32[]{:T(128)} %get-tuple-element.97, s32[4096]{0:T(1024)S(1)} %bitcast.234, s32[4096]{0:T(1024)S(1)} %bitcast.228, s32[4096]{0:T(1024)S(1)} %bitcast.229, s32[4096]{0:T(1024)S(1)} %bitcast.230, s32[4096]{0:T(1024)S(1)} %bitcast.231, ...), kind=kOutput, calls=%fused_computation.13.clone.1 | convolution fusion | flops 587202560 | bytes 1442816 | tf_op jit(solution)/shard_map/while/body/eval_jaxpr/dot_general | solution.py:20
  660.5 1.6 constant_dynamic-slice_fusion.9
  662.1 10.2 %fusion.43 = f32[16,512,128]{2,1,0:T(8,128)} fusion(f32[16,512,128]{2,1,0:T(8,128)} %get-tuple-element.98, s32[]{:T(128)} %get-tuple-element.97, s32[4096]{0:T(1024)S(1)} %bitcast.234, s32[4096]{0:T(1024)S(1)} %bitcast.228, s32[4096]{0:T(1024)S(1)} %bitcast.229, s32[4096]{0:T(1024)S(1)} %bitcast.230, s32[4096]{0:T(1024)S(1)} %bitcast.231, ...), kind=kOutput, calls=%fused_computation.13.clone.1 | convolution fusion | flops 587202560 | bytes 1442816 | tf_op jit(solution)/shard_map/while/body/eval_jaxpr/dot_general | solution.py:20
  672.3 1.9 constant_dynamic-slice_fusion.9
  674.2 10.2 %fusion.43 = f32[16,512,128]{2,1,0:T(8,128)} fusion(f32[16,512,128]{2,1,0:T(8,128)} %get-tuple-element.98, s32[]{:T(128)} %get-tuple-element.97, s32[4096]{0:T(1024)S(1)} %bitcast.234, s32[4096]{0:T(1024)S(1)} %bitcast.228, s32[4096]{0:T(1024)S(1)} %bitcast.229, s32[4096]{0:T(1024)S(1)} %bitcast.230, s32[4096]{0:T(1024)S(1)} %bitcast.231, ...), kind=kOutput, calls=%fused_computation.13.clone.1 | convolution fusion | flops 587202560 | bytes 1442816 | tf_op jit(solution)/shard_map/while/body/eval_jaxpr/dot_general | solution.py:20
  684.4 1.6 constant_dynamic-slice_fusion.9
  686.1 10.2 %fusion.43 = f32[16,512,128]{2,1,0:T(8,128)} fusion(f32[16,512,128]{2,1,0:T(8,128)} %get-tuple-element.98, s32[]{:T(128)} %get-tuple-element.97, s32[4096]{0:T(1024)S(1)} %bitcast.234, s32[4096]{0:T(1024)S(1)} %bitcast.228, s32[4096]{0:T(1024)S(1)} %bitcast.229, s32[4096]{0:T(1024)S(1)} %bitcast.230, s32[4096]{0:T(1024)S(1)} %bitcast.231, ...), kind=kOutput, calls=%fused_computation.13.clone.1 | convolution fusion | flops 587202560 | bytes 1442816 | tf_op jit(solution)/shard_map/while/body/eval_jaxpr/dot_general | solution.py:20
  696.2 3.3 multiply_reduce_fusion
  700.4 4.4 fusion.6
  704.8 7.5 all_gather.7
  712.3 77.8 %all-gather.2.cloned.1.call-done = bf16[64,512,128]{2,1,0:T(8,128)(2,1)} async-done(((bf16[16,512,128]{2,1,0:T(8,128)(2,1)}), bf16[64,512,128]{2,1,0:T(8,128)(2,1)}) %all-gather.2.cloned.1.call-update) | async-done | bytes 8388624 | tf_op jit(solution)/shard_map/all_gather | solution.py:70
  790.1 7.8 copy.134
  (46 shorter events, 35.1 us)
Async XLA Ops:
  20.7 99.9 %all-to-all-start = ((s32[128,512,8]{0,2,1:T(8,128)}), s32[128,512,8]{0,2,1:T(8,128)S(1)}, u32[]{:S(2)}, u32[]{:S(2)}) async-start(s32[128,512,8]{0,2,1:T(8,128)} %bitcast.225), calls=%async_computation | async-start | bytes 4194304 | tf_op jit(solution)/shard_map/all_to_all | solution.py:63
  120.7 370.5 %all-to-all-start.1 = ((bf16[32,128,16,128]{3,2,1,0:T(8,128)(2,1)}), bf16[32,128,16,128]{3,2,1,0:T(8,128)(2,1)}, u32[]{:S(2)}, u32[]{:S(2)}) async-start(bf16[32,128,16,128]{3,2,1,0:T(8,128)(2,1)} %fusion.8), calls=%async_computation.1 | async-start | bytes 33554432 | tf_op jit(solution)/shard_map/all_to_all | solution.py:55
  126.6 663.5 %all-gather.2.cloned.1.call-start = ((), (), s32[]{:S(2)}) async-start(), calls=%async_computation.2 | async-start | bytes 10485760 | tf_op jit(solution)/shard_map/all_gather | solution.py:70
Sparse Core Ops, SparseCore 0:
  704.9 85.1 all-gather.1
